TPU v7x, 32 devices: a whole 2x2x4 slice. The times are simulated.
32 devices in a mesh: row: 2 (over y), col: 4 (over z), depth: 4 (over x, core).
Axes of the slice: x: 2, y: 2, z: 4, core: 2. Of those that a mesh axis runs over, the one named last changes fastest.
Arguments:
- grad_out: bfloat16 [1024, 6144], P('depth', 'col'), may hold values from -6 to 6
- pre_act: bfloat16 [1024, 24576], P('depth', 'row'), may hold values from -8 to 8
- down_weight: bfloat16 [24576, 6144], P(('row', 'depth'), 'col'), may hold values from -0.0546875 to 0.0546875
Outputs:
- grad_pre: bfloat16 [1024, 24576], P('depth', 'row')
- grad_weight: bfloat16 [24576, 6144], P(('row', 'depth'), 'col')
All inputs are finite; a program needn't handle non-finite values.
Results may differ from a plain program's by a relative error of at most 0.0066.
Values may be sent and summed in bfloat16 or wider, within the bound.
A program may use at most 128 MiB of HBM per device.

v0:
```python
import functools

import jax
import jax.numpy as jnp
from jax import lax
from jax.experimental import pallas as pl
from jax.experimental.pallas import tpu as pltpu
from jax.sharding import PartitionSpec as P

MESH = pl.DeviceIdType.MESH
sqrt_two_pi = 0.7978845608028654
cubic_coeff = 0.044715
LAG = 2


def gelu_value(preact):
    tangent = jnp.tanh(sqrt_two_pi * (preact + cubic_coeff * preact * preact * preact))
    return 0.5 * preact * (1.0 + tangent)


def gelu_slope(preact):
    tangent = jnp.tanh(sqrt_two_pi * (preact + cubic_coeff * preact * preact * preact))
    inner = sqrt_two_pi * (1.0 + 3.0 * cubic_coeff * preact * preact)
    return 0.5 * (1.0 + tangent) + 0.5 * preact * (1.0 - tangent * tangent) * inner


def flip(a, b, extent):
    total, k = jnp.int32(0), 1
    while k < extent:
        bit = lax.div(a, jnp.int32(k)) + lax.div(b, jnp.int32(k))
        total = total + lax.rem(bit, jnp.int32(2)) * k
        k *= 2
    return total


def kernel(
    depths, width, grad_ref, pre_ref, weight_ref, out_ref, gw_ref,
    sums, from_edge, from_middle, pre, act, out, weight, grad,
    weight_sem, pre_sem, grad_sem, edge_sem, middle_sem, swap_sem, near_sem, far_sem,
    grad_send, sums_send, relay_send, swap_send, near_send, far_send, pass_send, pre_send,
    out_sem, gw_sem,
):
    col, place = lax.axis_index("col"), lax.axis_index("depth")
    rows, hidden = grad_ref.shape[0], weight_ref.shape[0]
    half = rows // 2
    tiles = hidden // width
    total = depths * tiles
    middle = (col == 1) | (col == 2)
    edge = (col == 0) | (col == 3)
    near = col + 1 - 2 * lax.rem(col, 2)
    across = 3 - col
    mine = pl.ds(pl.multiple_of(lax.rem(col + 1, 2) * half, half), half)
    theirs = pl.ds(pl.multiple_of(lax.rem(col, 2) * half, half), half)

    def columns(block, tile):
        return pl.ds(pl.multiple_of(block * hidden + tile * width, width), width)

    def to(axis, index):
        return {axis: index}

    def send(src, dst, send_sem, recv_sem, device):
        return pltpu.make_async_remote_copy(
            src_ref=src, dst_ref=dst, send_sem=send_sem, recv_sem=recv_sem,
            device_id=device, device_id_type=MESH,
        )

    def split(q):
        return lax.div(q, jnp.int32(tiles)), lax.rem(q, jnp.int32(tiles))

    def block_rows(s):
        return pl.ds(pl.multiple_of(s * rows, rows), rows)

    def load_weight(tile):
        return pltpu.make_async_copy(
            weight_ref.at[pl.ds(pl.multiple_of(tile * width, width), width), :],
            weight.at[tile], weight_sem.at[tile],
        )

    def load_pre(tile):
        return pltpu.make_async_copy(
            pre_ref.at[:, columns(place, tile)], pre.at[0, tile], pre_sem.at[tile]
        )

    def send_pre(s, tile):
        target = flip(place, s, depths)
        return send(
            pre_ref.at[:, columns(target, tile)], pre.at[s, tile], pre_send,
            pre_sem.at[s * tiles + tile], to("depth", target),
        )

    def load_grad():
        return pltpu.make_async_copy(grad_ref, grad.at[block_rows(0)], grad_sem.at[0])

    def send_grad(s):
        return send(
            grad_ref, grad.at[block_rows(s)], grad_send.at[s], grad_sem.at[s],
            to("depth", flip(place, jnp.int32(s), depths)),
        )

    def pass_grad(s):
        return send(
            grad.at[block_rows(s)], grad.at[block_rows(s + 1)], grad_send.at[s + 1],
            grad_sem.at[s + 1], to("depth", flip(place, jnp.int32(1), depths)),
        )

    def send_sums(q):
        return send(sums.at[q], from_edge.at[q], sums_send, edge_sem.at[q], to("col", near))

    def send_relay(q):
        return send(
            sums.at[q, theirs], from_middle.at[q], relay_send, middle_sem.at[q],
            to("col", across),
        )

    def send_swap(q):
        s, tile = split(q)
        return send(
            sums.at[q, mine], out.at[place, tile, mine], swap_send, swap_sem.at[q],
            to("depth", flip(place, s, depths)),
        )

    def send_out(q, which, send_sem, recv_sem, column):
        s, tile = split(q)
        part = out.at[flip(place, s, depths), tile, which]
        return send(part, part, send_sem, recv_sem.at[q], to("col", column))

    def store_out(q):
        s, tile = split(q)
        block = flip(place, s, depths)
        return pltpu.make_async_copy(
            out.at[block, tile], out_ref.at[:, columns(block, tile)], out_sem
        )

    def store_gw(tile):
        return pltpu.make_async_copy(
            weight.at[tile],
            gw_ref.at[pl.ds(pl.multiple_of(tile * width, width), width), :], gw_sem,
        )

    load_grad().start()
    load_weight(0).start()

    barrier = pltpu.get_barrier_semaphore()
    for s in range(1, depths):
        pl.semaphore_signal(
            barrier, inc=1, device_id=to("depth", flip(place, jnp.int32(s), depths)),
            device_id_type=MESH,
        )
    pl.semaphore_signal(barrier, inc=1, device_id=to("col", near), device_id_type=MESH)

    @pl.when(middle)
    def _():
        pl.semaphore_signal(barrier, inc=1, device_id=to("col", across), device_id_type=MESH)

    @pl.loop(1, tiles)
    def _(tile):
        load_weight(tile).start()

    @pl.loop(0, tiles)
    def _(tile):
        load_pre(tile).start()

    @pl.when(middle)
    def _():
        pl.semaphore_wait(barrier, depths + 1)

    @pl.when(edge)
    def _():
        pl.semaphore_wait(barrier, depths)

    send_grad(1).start()
    for s in range(2, depths, 2):
        send_grad(s).start()
    load_grad().wait()

    step_rows = 32

    def by_rows(count, body):
        @pl.loop(0, count // step_rows)
        def _(r):
            body(pl.ds(pl.multiple_of(r * step_rows, step_rows), step_rows), r)

    @pl.loop(0, total + 5 * LAG)
    def _(i):
        relayed, ended, swapped, passed, done = (i - k * LAG for k in range(1, 6))

        def at(q):
            return (q >= 0) & (q < total)

        @pl.when(middle & at(passed))
        def _():
            send_out(passed, theirs, far_send, far_sem, across).wait_recv()
            send_out(passed, theirs, pass_send, far_sem, near).start()

        @pl.when(middle & at(swapped))
        def _():
            @pl.when(swapped >= tiles)
            def _():
                send_swap(swapped).wait_recv()

            send_out(swapped, mine, near_send, near_sem, near).start()
            send_out(swapped, mine, far_send, far_sem, across).start()

        @pl.when(middle & at(relayed))
        def _():
            send_sums(relayed).wait_recv()
            base = lax.rem(col, 2) * half

            def body(_, r):
                lines = pl.ds(pl.multiple_of(base + r * step_rows, step_rows), step_rows)
                both = sums[relayed, lines, :].astype(jnp.float32)
                both += from_edge[relayed, lines, :].astype(jnp.float32)
                sums[relayed, lines, :] = both.astype(jnp.bfloat16)

            by_rows(half, body)
            send_relay(relayed).start()

        @pl.when(at(ended))
        def _():
            s, tile = split(ended)
            pltpu.make_async_copy(
                pre_ref.at[:, columns(place, tile)], pre.at[s, tile], pre_sem.at[ended]
            ).wait()

            @pl.when(middle)
            def _():
                send_relay(ended).wait_recv()
                base = lax.rem(col + 1, 2) * half

                def finish(r):
                    lines = pl.ds(pl.multiple_of(base + r * step_rows, step_rows), step_rows)
                    short = pl.ds(pl.multiple_of(r * step_rows, step_rows), step_rows)
                    back = sums[ended, lines, :].astype(jnp.float32)
                    back += from_edge[ended, lines, :].astype(jnp.float32)
                    back += from_middle[ended, short, :].astype(jnp.float32)
                    slope = gelu_slope(pre[s, tile, lines, :].astype(jnp.float32))
                    return lines, (back * slope).astype(jnp.bfloat16)

                @pl.when(ended < tiles)
                def _():
                    def body(_, r):
                        lines, value = finish(r)
                        out[place, tile, lines, :] = value

                    by_rows(half, body)

                @pl.when(ended >= tiles)
                def _():
                    def body(_, r):
                        lines, value = finish(r)
                        sums[ended, lines, :] = value

                    by_rows(half, body)
                    send_swap(ended).start()

        @pl.when(i < total)
        def _():
            s, tile = split(i)

            @pl.when(i < tiles)
            def _():
                load_weight(tile).wait()

            @pl.when((tile == 0) & (lax.rem(s, 2) == 1))
            def _():
                pltpu.make_async_copy(
                    grad_ref, grad.at[block_rows(s)], grad_sem.at[s]
                ).wait()

            sums[i] = lax.dot_general(
                grad[block_rows(s), :], weight[tile], (((1,), (1,)), ((), ())),
                preferred_element_type=jnp.float32,
            ).astype(jnp.bfloat16)

            @pl.when(edge)
            def _():
                send_sums(i).start()

        @pl.when(i < tiles)
        def _():
            send_pre(jnp.int32(1), i).start()

        turn = lax.div(i, 3) * 2 + lax.rem(i, 3)

        @pl.when((lax.rem(i, 3) < 2) & (turn < total - 2 * tiles))
        def _():
            s, tile = split(turn + 2 * tiles)
            send_pre(s, tile).start()

        @pl.when(i == tiles)
        def _():
            for s in range(2, depths, 2):
                send_grad(s).wait_recv()
                pass_grad(s).start()

        @pl.when(at(done))
        def _():
            @pl.when(edge)
            def _():
                send_out(done, theirs, near_send, near_sem, near).wait_recv()
                send_out(done, mine, far_send, far_sem, near).wait_recv()

            store_out(done).start()

        @pl.when(at(ended))
        def _():
            s, tile = split(ended)

            def body(lines, r):
                value = gelu_value(pre[s, tile, lines, :].astype(jnp.float32))
                where = pl.ds(pl.multiple_of(s * rows + r * step_rows, step_rows), step_rows)
                act[tile, where, :] = value.astype(jnp.bfloat16)

            by_rows(rows, body)

            @pl.when(ended >= total - tiles)
            def _():
                weight[tile] = lax.dot_general(
                    act[tile], grad[...], (((0,), (0,)), ((), ())),
                    preferred_element_type=jnp.float32,
                ).astype(jnp.bfloat16)
                store_gw(tile).start()

    pltpu.make_async_copy(weight, weight, gw_sem).wait()
    pltpu.make_async_copy(out, out, out_sem).wait()
    send_grad(1).wait_send()
    for s in range(2, depths, 2):
        send_grad(s).wait_send()
        pass_grad(s).wait_send()

    def drained(ref, sem):
        pltpu.make_async_copy(ref, ref, sem).wait()

    drained(pre.at[pl.ds(1, depths - 1)], pre_send)

    @pl.when(edge)
    def _():
        drained(sums, sums_send)

    @pl.when(middle)
    def _():
        drained(from_middle, relay_send)
        drained(from_middle.at[pl.ds(tiles, total - tiles)], swap_send)
        drained(from_middle, near_send)
        drained(from_middle, far_send)
        drained(from_middle, pass_send)


def solution(mesh):
    depths = mesh.shape["depth"]
    assert mesh.shape["col"] == 4

    def on_device(grad_out, pre_act, down_weight):
        rows, features = grad_out.shape
        hidden = down_weight.shape[0]
        width = 256 if hidden % 256 == 0 else 128
        tiles = hidden // width
        total = depths * tiles
        bf16 = jnp.bfloat16
        dma = pltpu.SemaphoreType.DMA
        anywhere = pl.BlockSpec(memory_space=pl.ANY)
        return pl.pallas_call(
            functools.partial(kernel, depths, width),
            out_shape=(
                jax.ShapeDtypeStruct(pre_act.shape, bf16),
                jax.ShapeDtypeStruct(down_weight.shape, bf16),
            ),
            in_specs=[anywhere] * 3,
            out_specs=(anywhere, anywhere),
            scratch_shapes=[
                pltpu.VMEM((total, rows, width), bf16),
                pltpu.VMEM((total, rows, width), bf16),
                pltpu.VMEM((total, rows // 2, width), bf16),
                pltpu.VMEM((depths, tiles, rows, width), bf16),
                pltpu.VMEM((tiles, depths * rows, width), bf16),
                pltpu.VMEM((depths, tiles, rows, width), bf16),
                pltpu.VMEM((tiles, width, features), bf16),
                pltpu.VMEM((depths * rows, features), bf16),
                dma((tiles,)), dma((total,)), dma((depths,)),
                dma((total,)), dma((total,)), dma((total,)), dma((total,)), dma((total,)),
                dma((depths,)), dma, dma, dma, dma, dma, dma, dma,
                dma, dma,
            ],
            compiler_params=pltpu.CompilerParams(
                collective_id=0, has_side_effects=True, vmem_limit_bytes=63 * 1024 * 1024
            ),
        )(grad_out, pre_act, down_weight)

    return jax.shard_map(
        on_device,
        mesh=mesh,
        in_specs=(P("depth", "col"), P("depth", "row"), P(("row", "depth"), "col")),
        out_specs=(P("depth", "row"), P(("row", "depth"), "col")),
        check_vma=False,
    )
```

profile of v0, /device:TPU:0, one launch (start us, length us, event | category | flops | bytes accessed | tf_op | source)
XLA Modules:
  0.0 180.5 jit_solution(12423538730539882075)
XLA Ops:
  0.6 165.7 %shard_map.50 = (bf16[256,12288]{1,0:T(8,128)(2,1)}, bf16[3072,1536]{1,0:T(8,128)(2,1)}) custom-call(bf16[256,1536]{1,0:T(8,128)(2,1)} %grad_ref.1, bf16[256,12288]{1,0:T(8,128)(2,1)} %pre_ref.1, bf16[3072,1536]{1,0:T(8,128)(2,1)} %weight_ref.1), custom_call_target="tpu_custom_call" | custom-call | tf_op jit(solution)/shard_map/pallas_call | solution.py:362
  166.4 6.1 %copy.7 = bf16[256,12288]{1,0:T(8,128)(2,1)} copy(bf16[256,12288]{1,0:T(8,128)(2,1)} %get-tuple-element.4) | data formatting | bytes 12582912
  172.5 8.0 %copy.8 = bf16[3072,1536]{1,0:T(8,128)(2,1)} copy(bf16[3072,1536]{1,0:T(8,128)(2,1)} %get-tuple-element.5) | data formatting | bytes 18874368
where the time goes:
time: 181 us
  Pallas kernels  166 us (92%)
  local copies, waits for them, and re-layouts  14.2 us (8%)
    pallas_call x1, Pallas kernels, on_device(): pl.pallas_call(functools.partial(kernel, depths, width), out_shape=(jax.S...  166 us
    unnamed x2, local copies, waits for them, and re-layouts  14.2 us

commit v1 on v0

--- a/solution.py
+++ b/solution.py
@@ -34,11 +34,10 @@
 
 
 def kernel(
-    depths, width, grad_ref, pre_ref, weight_ref, out_ref, gw_ref,
-    sums, from_edge, from_middle, pre, act, out, weight, grad,
+    depths, width, grad_ref, pre_ref, weight_ref, out, weight,
+    sums, from_edge, from_middle, pre, act, grad,
     weight_sem, pre_sem, grad_sem, edge_sem, middle_sem, swap_sem, near_sem, far_sem,
     grad_send, sums_send, relay_send, swap_send, near_send, far_send, pass_send, pre_send,
-    out_sem, gw_sem,
 ):
     col, place = lax.axis_index("col"), lax.axis_index("depth")
     rows, hidden = grad_ref.shape[0], weight_ref.shape[0]
@@ -70,10 +69,12 @@
     def block_rows(s):
         return pl.ds(pl.multiple_of(s * rows, rows), rows)
 
+    def tile_rows(tile):
+        return pl.ds(pl.multiple_of(tile * width, width), width)
+
     def load_weight(tile):
         return pltpu.make_async_copy(
-            weight_ref.at[pl.ds(pl.multiple_of(tile * width, width), width), :],
-            weight.at[tile], weight_sem.at[tile],
+            weight_ref.at[tile_rows(tile), :], weight.at[tile_rows(tile), :], weight_sem.at[tile]
         )
 
     def load_pre(tile):
@@ -115,27 +116,14 @@
     def send_swap(q):
         s, tile = split(q)
         return send(
-            sums.at[q, mine], out.at[place, tile, mine], swap_send, swap_sem.at[q],
+            sums.at[q, mine], out.at[mine, columns(place, tile)], swap_send, swap_sem.at[q],
             to("depth", flip(place, s, depths)),
         )
 
     def send_out(q, which, send_sem, recv_sem, column):
         s, tile = split(q)
-        part = out.at[flip(place, s, depths), tile, which]
+        part = out.at[which, columns(flip(place, s, depths), tile)]
         return send(part, part, send_sem, recv_sem.at[q], to("col", column))
-
-    def store_out(q):
-        s, tile = split(q)
-        block = flip(place, s, depths)
-        return pltpu.make_async_copy(
-            out.at[block, tile], out_ref.at[:, columns(block, tile)], out_sem
-        )
-
-    def store_gw(tile):
-        return pltpu.make_async_copy(
-            weight.at[tile],
-            gw_ref.at[pl.ds(pl.multiple_of(tile * width, width), width), :], gw_sem,
-        )
 
     load_grad().start()
     load_weight(0).start()
@@ -240,7 +228,7 @@
                 def _():
                     def body(_, r):
                         lines, value = finish(r)
-                        out[place, tile, lines, :] = value
+                        out[lines, columns(place, tile)] = value
 
                     by_rows(half, body)
 
@@ -268,7 +256,7 @@
                 ).wait()
 
             sums[i] = lax.dot_general(
-                grad[block_rows(s), :], weight[tile], (((1,), (1,)), ((), ())),
+                grad[block_rows(s), :], weight[tile_rows(tile), :], (((1,), (1,)), ((), ())),
                 preferred_element_type=jnp.float32,
             ).astype(jnp.bfloat16)
 
@@ -293,14 +281,10 @@
                 send_grad(s).wait_recv()
                 pass_grad(s).start()
 
-        @pl.when(at(done))
-        def _():
-            @pl.when(edge)
-            def _():
-                send_out(done, theirs, near_send, near_sem, near).wait_recv()
-                send_out(done, mine, far_send, far_sem, near).wait_recv()
-
-            store_out(done).start()
+        @pl.when(edge & at(done))
+        def _():
+            send_out(done, theirs, near_send, near_sem, near).wait_recv()
+            send_out(done, mine, far_send, far_sem, near).wait_recv()
 
         @pl.when(at(ended))
         def _():
@@ -315,14 +299,11 @@
 
             @pl.when(ended >= total - tiles)
             def _():
-                weight[tile] = lax.dot_general(
+                weight[tile_rows(tile), :] = lax.dot_general(
                     act[tile], grad[...], (((0,), (0,)), ((), ())),
                     preferred_element_type=jnp.float32,
                 ).astype(jnp.bfloat16)
-                store_gw(tile).start()
-
-    pltpu.make_async_copy(weight, weight, gw_sem).wait()
-    pltpu.make_async_copy(out, out, out_sem).wait()
+
     send_grad(1).wait_send()
     for s in range(2, depths, 2):
         send_grad(s).wait_send()
@@ -362,27 +343,24 @@
         return pl.pallas_call(
             functools.partial(kernel, depths, width),
             out_shape=(
-                jax.ShapeDtypeStruct(pre_act.shape, bf16),
-                jax.ShapeDtypeStruct(down_weight.shape, bf16),
+                pltpu.VMEM(pre_act.shape, bf16),
+                pltpu.VMEM(down_weight.shape, bf16),
             ),
             in_specs=[anywhere] * 3,
-            out_specs=(anywhere, anywhere),
+            out_specs=(pl.BlockSpec(memory_space=pltpu.VMEM),) * 2,
             scratch_shapes=[
                 pltpu.VMEM((total, rows, width), bf16),
                 pltpu.VMEM((total, rows, width), bf16),
                 pltpu.VMEM((total, rows // 2, width), bf16),
                 pltpu.VMEM((depths, tiles, rows, width), bf16),
                 pltpu.VMEM((tiles, depths * rows, width), bf16),
-                pltpu.VMEM((depths, tiles, rows, width), bf16),
-                pltpu.VMEM((tiles, width, features), bf16),
                 pltpu.VMEM((depths * rows, features), bf16),
                 dma((tiles,)), dma((total,)), dma((depths,)),
                 dma((total,)), dma((total,)), dma((total,)), dma((total,)), dma((total,)),
                 dma((depths,)), dma, dma, dma, dma, dma, dma, dma,
-                dma, dma,
             ],
             compiler_params=pltpu.CompilerParams(
-                collective_id=0, has_side_effects=True, vmem_limit_bytes=63 * 1024 * 1024
+                collective_id=0, has_side_effects=True, vmem_limit_bytes=40 * 1024 * 1024
             ),
         )(grad_out, pre_act, down_weight)
 

time: 181 us -> 172 us (0.950)
  local copies, waits for them, and re-layouts: 14.2 us -> 6.45 us
    unnamed x2, local copies, waits for them, and re-layouts: 14.2 us -> 6.45 us
where the time goes in v1:
time: 172 us
  Pallas kernels  165 us (96%)
  local copies, waits for them, and re-layouts  6.45 us (4%)
    pallas_call x1, Pallas kernels, on_device(): pl.pallas_call(functools.partial(kernel, depths, width), out_shape=(pltpu...  165 us
    unnamed x2, local copies, waits for them, and re-layouts  6.45 us

profile of v1, /device:TPU:0, one launch (start us, length us, event | category | flops | bytes accessed | tf_op | source)
XLA Modules:
  0.0 172.1 jit_solution(12393909595405766504)
XLA Ops:
  0.6 165.0 %shard_map.50 = (bf16[256,12288]{1,0:T(8,128)(2,1)S(1)}, bf16[3072,1536]{1,0:T(8,128)(2,1)S(1)}) custom-call(bf16[256,1536]{1,0:T(8,128)(2,1)} %grad_ref.1, bf16[256,12288]{1,0:T(8,128)(2,1)} %pre_ref.1, bf16[3072,1536]{1,0:T(8,128)(2,1)} %weight_ref.1), custom_call_target="tpu_custom_call" | custom-call | tf_op jit(solution)/shard_map/pallas_call | solution.py:343
  165.7 2.7 %copy.7 = bf16[256,12288]{1,0:T(8,128)(2,1)} copy(bf16[256,12288]{1,0:T(8,128)(2,1)S(1)} %get-tuple-element.2) | data formatting | bytes 12582912
  168.4 3.7 %copy.8 = bf16[3072,1536]{1,0:T(8,128)(2,1)} copy(bf16[3072,1536]{1,0:T(8,128)(2,1)S(1)} %get-tuple-element.3) | data formatting | bytes 18874368

commit v2 on v1

v2 whole, which is shorter than its diff:
```python
import functools

import jax
import jax.numpy as jnp
from jax import lax
from jax.experimental import pallas as pl
from jax.experimental.pallas import tpu as pltpu
from jax.sharding import PartitionSpec as P

MESH = pl.DeviceIdType.MESH
sqrt_two_pi = 0.7978845608028654
cubic_coeff = 0.044715
PARTS = 1
RELAY, PAIR, SWAP, PASS = 1, 1, 2, 1
TAIL = -(-(RELAY + 1) // PARTS)


def gelu_value(preact):
    tangent = jnp.tanh(sqrt_two_pi * (preact + cubic_coeff * preact * preact * preact))
    return 0.5 * preact * (1.0 + tangent)


def gelu_slope(preact):
    tangent = jnp.tanh(sqrt_two_pi * (preact + cubic_coeff * preact * preact * preact))
    inner = sqrt_two_pi * (1.0 + 3.0 * cubic_coeff * preact * preact)
    return 0.5 * (1.0 + tangent) + 0.5 * preact * (1.0 - tangent * tangent) * inner


def flip(a, b, extent):
    total, k = jnp.int32(0), 1
    while k < extent:
        bit = lax.div(a, jnp.int32(k)) + lax.div(b, jnp.int32(k))
        total = total + lax.rem(bit, jnp.int32(2)) * k
        k *= 2
    return total


def kernel(
    depths, width, grad_ref, pre_ref, weight_ref, out, weight,
    sums, from_edge, from_middle, pre, act, grad,
    weight_sem, pre_sem, grad_sem, edge_sem, middle_sem, swap_sem, far_sem, near_sem, pass_sem,
    grad_send, sums_send, relay_send, swap_send, near_send, far_send, pass_send, pre_send,
):
    col, place = lax.axis_index("col"), lax.axis_index("depth")
    rows, hidden = grad_ref.shape[0], weight_ref.shape[0]
    span = rows // PARTS
    half = span // 2
    tiles = hidden // width
    first = tiles - TAIL
    total = depths * tiles
    units = total * PARTS
    distant = total - 2 * tiles
    burst = 3 * distant // 4
    rest = max(burst, 2 * tiles)
    gap = max(g for g in (1, 2, 3) if rest + g * (distant - 1 - burst) < total - TAIL - 1 or g == 1)
    middle = (col == 1) | (col == 2)
    edge = (col == 0) | (col == 3)
    near = col + 1 - 2 * lax.rem(col, 2)
    across = 3 - col
    mine, theirs = lax.rem(col + 1, 2) * half, lax.rem(col, 2) * half

    def div(a, b):
        return lax.div(a, jnp.int32(b))

    def rem(a, b):
        return lax.rem(a, jnp.int32(b))

    def columns(block, tile):
        return pl.ds(pl.multiple_of(block * hidden + tile * width, width), width)

    def send(src, dst, send_sem, recv_sem, axis, index):
        return pltpu.make_async_remote_copy(
            src_ref=src, dst_ref=dst, send_sem=send_sem, recv_sem=recv_sem,
            device_id={axis: index}, device_id_type=MESH,
        )

    def block_tile(t):
        later = t - first + tiles
        others = (t >= first) & (t < total - TAIL)
        s = jnp.where(others, div(later, tiles), 0)
        tile = jnp.where(others, rem(later, tiles), jnp.where(t < first, t, t - total + tiles))
        return s, tile

    def unit(u):
        t = div(u, PARTS)
        s, tile = block_tile(t)
        return t, s, tile, rem(u, PARTS) * span

    def lines(start, count):
        return pl.ds(pl.multiple_of(start, count), count)

    def block_rows(s):
        return lines(s * rows, rows)

    def tile_rows(tile):
        return lines(tile * width, width)

    def load_weight(tile):
        return pltpu.make_async_copy(
            weight_ref.at[tile_rows(tile), :], weight.at[tile_rows(tile), :], weight_sem.at[tile]
        )

    def load_pre(s, tile):
        return pltpu.make_async_copy(
            pre_ref.at[:, columns(place, tile)], pre.at[s, tile], pre_sem.at[s * tiles + tile]
        )

    def send_pre(s, tile):
        target = flip(place, s, depths)
        return send(
            pre_ref.at[:, columns(target, tile)], pre.at[s, tile], pre_send,
            pre_sem.at[s * tiles + tile], "depth", target,
        )

    def load_grad(s):
        return pltpu.make_async_copy(grad_ref, grad.at[block_rows(s)], grad_sem.at[s])

    def send_grad(s):
        return send(
            grad_ref, grad.at[block_rows(s)], grad_send.at[s], grad_sem.at[s],
            "depth", flip(place, jnp.int32(s), depths),
        )

    def pass_grad(s):
        return send(
            grad.at[block_rows(s)], grad.at[block_rows(s + 1)], grad_send.at[s + 1],
            grad_sem.at[s + 1], "depth", flip(place, jnp.int32(1), depths),
        )

    def send_sums(u):
        t, _, _, base = unit(u)
        which = lines(base, span)
        return send(
            sums.at[t, which], from_edge.at[t, which], sums_send, edge_sem.at[u], "col", near
        )

    def send_relay(u):
        t, _, _, base = unit(u)
        return send(
            sums.at[t, lines(base + theirs, half)], from_middle.at[u], relay_send,
            middle_sem.at[u], "col", across,
        )

    def send_swap(u):
        t, s, tile, base = unit(u)
        which = lines(base + mine, half)
        return send(
            sums.at[t, which], out.at[which, columns(place, tile)], swap_send, swap_sem.at[u],
            "depth", flip(place, s, depths),
        )

    def send_out(u, part, send_sem, recv_sem, column):
        _, s, tile, base = unit(u)
        piece = out.at[lines(base + part, half), columns(flip(place, s, depths), tile)]
        return send(piece, piece, send_sem, recv_sem, "col", column)

    load_grad(0).start()
    load_weight(0).start()

    barrier = pltpu.get_barrier_semaphore()
    for s in range(1, depths):
        pl.semaphore_signal(
            barrier, inc=1, device_id={"depth": flip(place, jnp.int32(s), depths)},
            device_id_type=MESH,
        )
    pl.semaphore_signal(barrier, inc=1, device_id={"col": near}, device_id_type=MESH)

    @pl.when(middle)
    def _():
        pl.semaphore_signal(barrier, inc=1, device_id={"col": across}, device_id_type=MESH)

    @pl.loop(1, tiles)
    def _(tile):
        load_weight(tile).start()

    @pl.loop(0, tiles)
    def _(tile):
        load_pre(0, tile).start()

    @pl.when(middle)
    def _():
        pl.semaphore_wait(barrier, depths + 1)

    @pl.when(edge)
    def _():
        pl.semaphore_wait(barrier, depths)

    send_grad(1).start()
    for s in range(2, depths, 2):
        send_grad(s).start()
    load_grad(0).wait()

    step = 32

    def by_rows(count, body):
        @pl.loop(0, count // step)
        def _(r):
            body(r * step)

    def give_out(u):
        send_out(u, mine, near_send, near_sem, near).start()
        send_out(u, mine, far_send, far_sem.at[u], across).start()

    def pass_out(u):
        send_out(u, theirs, far_send, far_sem.at[u], across).wait_recv()
        send_out(u, theirs, pass_send, pass_sem, near).start()

    def own_tokens(u):
        return ((u >= 0) & (u < first * PARTS)) | ((u >= units - TAIL * PARTS) & (u < units))

    def pair_tokens(u):
        return (u >= first * PARTS) & (u < (first + tiles) * PARTS)

    def far_tokens(u):
        return (u >= (first + tiles) * PARTS) & (u < units - TAIL * PARTS)

    @pl.loop(0, units + 1 + RELAY + SWAP + PASS)
    def _(i):
        relayed = i - 1
        ended = relayed - RELAY
        @pl.when(middle & (relayed >= 0) & (relayed < units))
        def _():
            send_sums(relayed).wait_recv()
            t, _, _, base = unit(relayed)

            def body(r):
                which = lines(base + theirs + r, step)
                both = sums[t, which, :].astype(jnp.float32)
                both += from_edge[t, which, :].astype(jnp.float32)
                sums[t, which, :] = both.astype(jnp.bfloat16)

            by_rows(half, body)
            send_relay(relayed).start()

        @pl.when((ended >= 0) & (ended < units))
        def _():
            t, s, tile, base = unit(ended)

            @pl.when((s > 0) & (base == 0))
            def _():
                load_pre(s, tile).wait()

            @pl.when(middle)
            def _():
                send_relay(ended).wait_recv()

                def finish(r):
                    which = lines(base + mine + r, step)
                    back = sums[t, which, :].astype(jnp.float32)
                    back += from_edge[t, which, :].astype(jnp.float32)
                    back += from_middle[ended, lines(r, step), :].astype(jnp.float32)
                    slope = gelu_slope(pre[s, tile, which, :].astype(jnp.float32))
                    return which, (back * slope).astype(jnp.bfloat16)

                @pl.when(s == 0)
                def _():
                    def body(r):
                        which, value = finish(r)
                        out[which, columns(place, tile)] = value

                    by_rows(half, body)
                    give_out(ended)

                @pl.when(s > 0)
                def _():
                    def body(r):
                        which, value = finish(r)
                        sums[t, which, :] = value

                    by_rows(half, body)
                    send_swap(ended).start()

        @pl.when(middle & pair_tokens(ended - PAIR))
        def _():
            send_swap(ended - PAIR).wait_recv()
            give_out(ended - PAIR)

        @pl.when(middle & far_tokens(ended - SWAP))
        def _():
            send_swap(ended - SWAP).wait_recv()
            give_out(ended - SWAP)

        turn = div(i, PARTS)

        @pl.when((rem(i, PARTS) == 0) & (i < units))
        def _():
            s, tile = block_tile(turn)

            @pl.when((turn < first) | ((s == 1) & (tile >= first)))
            def _():
                load_weight(tile).wait()

            @pl.when((tile == 0) & (rem(s, 2) == 1))
            def _():
                load_grad(s).wait()

            sums[turn] = lax.dot_general(
                grad[block_rows(s), :], weight[tile_rows(tile), :], (((1,), (1,)), ((), ())),
                preferred_element_type=jnp.float32,
            ).astype(jnp.bfloat16)

            @pl.when(edge)
            def _():
                for part in range(PARTS):
                    send_sums(i + part).start()

            @pl.when(turn < tiles)
            def _():
                send_pre(jnp.int32(1), turn).start()

            def push(k):
                send_pre(2 + div(k, tiles), rem(k, tiles)).start()

            @pl.when(turn < burst)
            def _():
                push(turn)

            after = turn - rest
            slow = burst + div(after, gap)

            @pl.when((after >= 0) & (rem(after, gap) == 0) & (slow < distant))
            def _():
                push(slow)

            @pl.when(turn == tiles)
            def _():
                for s in range(2, depths, 2):
                    send_grad(s).wait_recv()
                    pass_grad(s).start()

            block, slot = div(turn, tiles), rem(turn, tiles)

            @pl.when(block == 0)
            def _():
                load_pre(0, slot).wait()

            def body(r):
                value = gelu_value(pre[block, slot, lines(r, step), :].astype(jnp.float32))
                act[slot, lines(block * rows + r, step), :] = value.astype(jnp.bfloat16)

            by_rows(rows, body)

            @pl.when(block == depths - 1)
            def _():
                weight[tile_rows(slot), :] = lax.dot_general(
                    act[slot], grad[...], (((0,), (0,)), ((), ())),
                    preferred_element_type=jnp.float32,
                ).astype(jnp.bfloat16)

        for among, lag in ((far_tokens, SWAP), (pair_tokens, PAIR), (own_tokens, 0)):
            @pl.when(middle & among(ended - lag - PASS))
            def _():
                pass_out(ended - lag - PASS)

    send_grad(1).wait_send()
    for s in range(2, depths, 2):
        send_grad(s).wait_send()
        pass_grad(s).wait_send()

    def drained(ref, sem):
        pltpu.make_async_copy(ref, ref, sem).wait()

    drained(pre.at[pl.ds(1, depths - 1)], pre_send)

    @pl.when(edge)
    def _():
        drained(sums, sums_send)
        drained(from_middle, near_sem)
        drained(from_middle, pass_sem)

    @pl.when(middle)
    def _():
        drained(from_middle, relay_send)
        drained(from_middle.at[pl.ds(0, units - tiles * PARTS)], swap_send)
        drained(from_middle, near_send)
        drained(from_middle, far_send)
        drained(from_middle, pass_send)


def write_out(results):
    parts = 4

    def body(first, second, first_out, second_out, sems):
        copies = []
        for k in range(parts):
            for n, (src, dst) in enumerate(((first, first_out), (second, second_out))):
                size = src.shape[0] // parts
                piece = pl.ds(k * size, size)
                copies.append(pltpu.make_async_copy(src.at[piece], dst.at[piece], sems.at[n, k]))
        for copy in copies:
            copy.start()
        for copy in copies:
            copy.wait()

    anywhere = pl.BlockSpec(memory_space=pl.ANY)
    return pl.pallas_call(
        body,
        out_shape=tuple(jax.ShapeDtypeStruct(r.shape, r.dtype) for r in results),
        in_specs=[pl.BlockSpec(memory_space=pltpu.VMEM)] * 2,
        out_specs=(anywhere, anywhere),
        scratch_shapes=[pltpu.SemaphoreType.DMA((2, parts))],
        compiler_params=pltpu.CompilerParams(vmem_limit_bytes=20 * 1024 * 1024),
    )(*results)


def solution(mesh):
    depths = mesh.shape["depth"]
    assert mesh.shape["col"] == 4

    def on_device(grad_out, pre_act, down_weight):
        rows, features = grad_out.shape
        hidden = down_weight.shape[0]
        width = 256 if hidden % 256 == 0 else 128
        tiles = hidden // width
        total = depths * tiles
        units = total * PARTS
        bf16 = jnp.bfloat16
        dma = pltpu.SemaphoreType.DMA
        anywhere = pl.BlockSpec(memory_space=pl.ANY)
        results = pl.pallas_call(
            functools.partial(kernel, depths, width),
            out_shape=(
                pltpu.VMEM(pre_act.shape, bf16),
                pltpu.VMEM(down_weight.shape, bf16),
            ),
            in_specs=[anywhere] * 3,
            out_specs=(pl.BlockSpec(memory_space=pltpu.VMEM),) * 2,
            scratch_shapes=[
                pltpu.VMEM((total, rows, width), bf16),
                pltpu.VMEM((total, rows, width), bf16),
                pltpu.VMEM((total * PARTS, rows // PARTS // 2, width), bf16),
                pltpu.VMEM((depths, tiles, rows, width), bf16),
                pltpu.VMEM((tiles, depths * rows, width), bf16),
                pltpu.VMEM((depths * rows, features), bf16),
                dma((tiles,)), dma((total,)), dma((depths,)),
                dma((units,)), dma((units,)), dma((units,)), dma((units,)), dma, dma,
                dma((depths,)), dma, dma, dma, dma, dma, dma, dma,
            ],
            compiler_params=pltpu.CompilerParams(
                collective_id=0, has_side_effects=True, vmem_limit_bytes=40 * 1024 * 1024
            ),
        )(grad_out, pre_act, down_weight)
        return write_out(results)

    return jax.shard_map(
        on_device,
        mesh=mesh,
        in_specs=(P("depth", "col"), P("depth", "row"), P(("row", "depth"), "col")),
        out_specs=(P("depth", "row"), P(("row", "depth"), "col")),
        check_vma=False,
    )
```

time: 172 us -> 166 us (0.965)
  local copies, waits for them, and re-layouts: 6.45 us -> 0 us
    unnamed x2 -> x0, local copies, waits for them, and re-layouts: 6.45 us -> none
    pallas_call x0 -> x1, Pallas kernels: none -> 5.65 us  [write_out(): pl.pallas_call(body, out_shape=tuple((jax.ShapeDtypeStruct(r.shape, r.dty...]
    pallas_call x1, Pallas kernels: 165 us -> 160 us  [on_device(): pl.pallas_call(functools.partial(kernel, depths, width), out_shape=(pltpu...]
where the time goes in v2:
time: 166 us
  Pallas kernels  165 us (99%)
    pallas_call x1, Pallas kernels, on_device(): pl.pallas_call(functools.partial(kernel, depths, width), out_shape=(pltpu...  160 us
    pallas_call x1, Pallas kernels, write_out(): pl.pallas_call(body, out_shape=tuple((jax.ShapeDtypeStruct(r.shape, r.dty...  5.65 us

profile of v2, /device:TPU:0, one launch (start us, length us, event | category | flops | bytes accessed | tf_op | source)
XLA Modules:
  0.0 166.1 jit_solution(6825425049975932863)
XLA Ops:
  0.6 159.8 %shard_map.50 = (bf16[256,12288]{1,0:T(8,128)(2,1)S(1)}, bf16[3072,1536]{1,0:T(8,128)(2,1)S(1)}) custom-call(bf16[256,1536]{1,0:T(8,128)(2,1)} %grad_ref.1, bf16[256,12288]{1,0:T(8,128)(2,1)} %pre_ref.1, bf16[3072,1536]{1,0:T(8,128)(2,1)} %weight_ref.1), custom_call_target="tpu_custom_call" | custom-call | tf_op jit(solution)/shard_map/pallas_call | solution.py:420
  160.4 5.7 %shard_map.51 = (bf16[256,12288]{1,0:T(8,128)(2,1)}, bf16[3072,1536]{1,0:T(8,128)(2,1)}) custom-call(bf16[256,12288]{1,0:T(8,128)(2,1)S(1)} %get-tuple-element.4.first, bf16[3072,1536]{1,0:T(8,128)(2,1)S(1)} %get-tuple-element.5.second), custom_call_target="tpu_custom_call" | custom-call | tf_op jit(solution)/shard_map/pallas_call | solution.py:396

commit v3 on v2

v3 whole, which is shorter than its diff:
```python
import functools

import jax
import jax.numpy as jnp
from jax import lax
from jax.experimental import pallas as pl
from jax.experimental.pallas import tpu as pltpu
from jax.sharding import PartitionSpec as P

MESH = pl.DeviceIdType.MESH
sqrt_two_pi = 0.7978845608028654
cubic_coeff = 0.044715
HOP = 3
FINISH = 12


def gelu_value(preact):
    tangent = jnp.tanh(sqrt_two_pi * (preact + cubic_coeff * preact * preact * preact))
    return 0.5 * preact * (1.0 + tangent)


def gelu_slope(preact):
    tangent = jnp.tanh(sqrt_two_pi * (preact + cubic_coeff * preact * preact * preact))
    inner = sqrt_two_pi * (1.0 + 3.0 * cubic_coeff * preact * preact)
    return 0.5 * (1.0 + tangent) + 0.5 * preact * (1.0 - tangent * tangent) * inner


def flip(a, b, extent):
    total, k = jnp.int32(0), 1
    while k < extent:
        bit = lax.div(a, jnp.int32(k)) + lax.div(b, jnp.int32(k))
        total = total + lax.rem(bit, jnp.int32(2)) * k
        k *= 2
    return total


def kernel(
    depths, width, grad_ref, pre_ref, weight_ref, out, weight,
    sums, from_near, from_across, pre, act, grad,
    weight_sem, pre_sem, grad_sem, near_sem, across_sem, swap_sem, give_sem, far_sem, pass_sem,
    grad_send, near_send, across_send, swap_send, give_send, far_send, pass_send, pre_send,
):
    col, place = lax.axis_index("col"), lax.axis_index("depth")
    rows, hidden = grad_ref.shape[0], weight_ref.shape[0]
    half = rows // 2
    tiles = hidden // width
    total = depths * tiles
    middle = (col == 1) | (col == 2)
    edge = (col == 0) | (col == 3)
    near = col + 1 - 2 * lax.rem(col, 2)
    across = 3 - col
    mine = pl.multiple_of(lax.rem(col + 1, 2) * half, half)
    theirs = pl.multiple_of(lax.rem(col, 2) * half, half)

    def split(q):
        return lax.div(q, jnp.int32(tiles)), lax.rem(q, jnp.int32(tiles))

    def columns(block, tile):
        return pl.ds(pl.multiple_of(block * hidden + tile * width, width), width)

    def lines(start, count):
        return pl.ds(pl.multiple_of(start, count), count)

    def block_rows(s):
        return lines(s * rows, rows)

    def tile_rows(tile):
        return lines(tile * width, width)

    def send(src, dst, send_sem, recv_sem, axis, index):
        return pltpu.make_async_remote_copy(
            src_ref=src, dst_ref=dst, send_sem=send_sem, recv_sem=recv_sem,
            device_id={axis: index}, device_id_type=MESH,
        )

    def load_weight(tile):
        return pltpu.make_async_copy(
            weight_ref.at[tile_rows(tile), :], weight.at[tile_rows(tile), :], weight_sem.at[tile]
        )

    def load_pre(s, tile):
        return pltpu.make_async_copy(
            pre_ref.at[:, columns(place, tile)], pre.at[s, tile], pre_sem.at[s * tiles + tile]
        )

    def send_pre(s, tile):
        target = flip(place, s, depths)
        return send(
            pre_ref.at[:, columns(target, tile)], pre.at[s, tile], pre_send,
            pre_sem.at[s * tiles + tile], "depth", target,
        )

    def load_grad(s):
        return pltpu.make_async_copy(grad_ref, grad.at[block_rows(s)], grad_sem.at[s])

    def send_grad(s):
        return send(
            grad_ref, grad.at[block_rows(s)], grad_send.at[s], grad_sem.at[s],
            "depth", flip(place, jnp.int32(s), depths),
        )

    def pass_grad(s):
        return send(
            grad.at[block_rows(s)], grad.at[block_rows(s + 1)], grad_send.at[s + 1],
            grad_sem.at[s + 1], "depth", flip(place, jnp.int32(1), depths),
        )

    def send_near(q):
        return send(
            sums.at[q, lines(mine, half)], from_near.at[q], near_send, near_sem.at[q], "col", near
        )

    def send_across(q):
        return send(
            sums.at[q, lines(theirs, half)], from_across.at[q], across_send, across_sem.at[q],
            "col", across,
        )

    def send_swap(q):
        s, tile = split(q)
        which = lines(theirs, half)
        return send(
            sums.at[q, which], out.at[which, columns(place, tile)], swap_send, swap_sem.at[q],
            "depth", flip(place, s, depths),
        )

    def send_out(q, part, send_sem, recv_sem, column):
        s, tile = split(q)
        piece = out.at[lines(part, half), columns(flip(place, s, depths), tile)]
        return send(piece, piece, send_sem, recv_sem, "col", column)

    load_grad(0).start()
    load_weight(0).start()

    barrier = pltpu.get_barrier_semaphore()
    for s in range(1, depths):
        pl.semaphore_signal(
            barrier, inc=1, device_id={"depth": flip(place, jnp.int32(s), depths)},
            device_id_type=MESH,
        )
    pl.semaphore_signal(barrier, inc=1, device_id={"col": near}, device_id_type=MESH)

    @pl.when(middle)
    def _():
        pl.semaphore_signal(barrier, inc=1, device_id={"col": across}, device_id_type=MESH)

    @pl.loop(1, tiles)
    def _(tile):
        load_weight(tile).start()

    @pl.loop(0, tiles)
    def _(tile):
        load_pre(0, tile).start()

    @pl.when(middle)
    def _():
        pl.semaphore_wait(barrier, depths + 1)

    @pl.when(edge)
    def _():
        pl.semaphore_wait(barrier, depths)

    send_grad(1).start()
    for s in range(2, depths, 2):
        send_grad(s).start()
    load_grad(0).wait()

    step = 32

    def by_rows(count, body):
        @pl.loop(0, count // step)
        def _(r):
            body(r * step)

    def at(q):
        return (q >= 0) & (q < total)

    def add_into(q, part, other):
        def body(r):
            which = lines(part + r, step)
            both = sums[q, which, :].astype(jnp.float32)
            both += other[q, lines(r, step), :].astype(jnp.float32)
            sums[q, which, :] = both.astype(jnp.bfloat16)

        by_rows(half, body)

    turns = max(2 * total + 1 + HOP, total + FINISH + 2 * tiles)

    @pl.loop(0, turns)
    def _(i):
        inward = i - 1
        outward = inward - HOP
        ended = i - FINISH
        given = i - total
        spread = given - 1
        passed = spread - HOP

        @pl.when(middle & at(inward))
        def _():
            send_near(inward).wait_recv()
            add_into(inward, theirs, from_near)
            send_across(inward).start()

        @pl.when(middle & at(outward))
        def _():
            send_across(outward).wait_recv()
            add_into(outward, mine, from_across)
            send_near(outward).start()

        @pl.when(middle & at(spread))
        def _():
            send_out(spread, mine, give_send, give_sem.at[spread], near).wait_recv()
            send_out(spread, mine, far_send, far_sem.at[spread], across).start()

        @pl.when(middle & at(passed))
        def _():
            send_out(passed, theirs, far_send, far_sem.at[passed], across).wait_recv()
            send_out(passed, theirs, pass_send, pass_sem, near).start()

        @pl.when(edge & at(given))
        def _():
            @pl.when(given >= tiles)
            def _():
                send_swap(given).wait_recv()

            send_out(given, theirs, give_send, give_sem.at[given], near).start()

        @pl.when(i < total)
        def _():
            s, tile = split(i)

            @pl.when(s == 0)
            def _():
                load_weight(tile).wait()

            @pl.when((tile == 0) & (lax.rem(s, jnp.int32(2)) == 1))
            def _():
                load_grad(s).wait()

            sums[i] = lax.dot_general(
                grad[block_rows(s), :], weight[tile_rows(tile), :], (((1,), (1,)), ((), ())),
                preferred_element_type=jnp.float32,
            ).astype(jnp.bfloat16)

            @pl.when(edge)
            def _():
                send_near(i).start()

        @pl.when(i < tiles)
        def _():
            send_pre(jnp.int32(1), i).start()

        @pl.when(i < total - 2 * tiles)
        def _():
            s, tile = split(i)
            send_pre(s + 2, tile).start()

        @pl.when(i == tiles + tiles // 2)
        def _():
            for s in range(2, depths, 2):
                send_grad(s).wait_recv()
                pass_grad(s).start()

        @pl.when(at(ended))
        def _():
            s, tile = split(ended)
            load_pre(s, tile).wait()

            @pl.when(edge)
            def _():
                send_near(ended).wait_recv()

                def finish(r):
                    which = lines(theirs + r, step)
                    back = sums[ended, which, :].astype(jnp.float32)
                    back += from_near[ended, lines(r, step), :].astype(jnp.float32)
                    slope = gelu_slope(pre[s, tile, which, :].astype(jnp.float32))
                    return which, (back * slope).astype(jnp.bfloat16)

                @pl.when(s == 0)
                def _():
                    def body(r):
                        which, value = finish(r)
                        out[which, columns(place, tile)] = value

                    by_rows(half, body)

                @pl.when(s > 0)
                def _():
                    def body(r):
                        which, value = finish(r)
                        sums[ended, which, :] = value

                    by_rows(half, body)
                    send_swap(ended).start()

            def body(r):
                value = gelu_value(pre[s, tile, lines(r, step), :].astype(jnp.float32))
                act[tile, lines(s * rows + r, step), :] = value.astype(jnp.bfloat16)

            by_rows(rows, body)

        late = i - total - FINISH

        @pl.when((late >= 0) & (lax.rem(late, 2) == 0) & (late < 2 * tiles))
        def _():
            tile = lax.div(late, 2)
            weight[tile_rows(tile), :] = lax.dot_general(
                act[tile], grad[...], (((0,), (0,)), ((), ())),
                preferred_element_type=jnp.float32,
            ).astype(jnp.bfloat16)

    send_grad(1).wait_send()
    for s in range(2, depths, 2):
        send_grad(s).wait_send()
        pass_grad(s).wait_send()

    def drained(ref, sem):
        pltpu.make_async_copy(ref, ref, sem).wait()

    drained(pre.at[pl.ds(1, depths - 1)], pre_send)
    drained(from_near, near_send)

    @pl.when(edge)
    def _():
        drained(from_near.at[pl.ds(tiles, total - tiles)], swap_send)
        drained(from_near, give_send)
        drained(from_near, pass_sem)

    @pl.when(middle)
    def _():
        drained(from_near, across_send)
        drained(from_near, far_send)
        drained(from_near, pass_send)


def write_out(results):
    parts = 4

    def body(first, second, first_out, second_out, sems):
        copies = []
        for k in range(parts):
            for n, (src, dst) in enumerate(((first, first_out), (second, second_out))):
                size = src.shape[0] // parts
                piece = pl.ds(k * size, size)
                copies.append(pltpu.make_async_copy(src.at[piece], dst.at[piece], sems.at[n, k]))
        for copy in copies:
            copy.start()
        for copy in copies:
            copy.wait()

    anywhere = pl.BlockSpec(memory_space=pl.ANY)
    return pl.pallas_call(
        body,
        out_shape=tuple(jax.ShapeDtypeStruct(r.shape, r.dtype) for r in results),
        in_specs=[pl.BlockSpec(memory_space=pltpu.VMEM)] * 2,
        out_specs=(anywhere, anywhere),
        scratch_shapes=[pltpu.SemaphoreType.DMA((2, parts))],
        compiler_params=pltpu.CompilerParams(vmem_limit_bytes=20 * 1024 * 1024),
    )(*results)


def solution(mesh):
    depths = mesh.shape["depth"]
    assert mesh.shape["col"] == 4

    def on_device(grad_out, pre_act, down_weight):
        rows, features = grad_out.shape
        hidden = down_weight.shape[0]
        width = 256 if hidden % 256 == 0 else 128
        tiles = hidden // width
        total = depths * tiles
        bf16 = jnp.bfloat16
        dma = pltpu.SemaphoreType.DMA
        anywhere = pl.BlockSpec(memory_space=pl.ANY)
        results = pl.pallas_call(
            functools.partial(kernel, depths, width),
            out_shape=(
                pltpu.VMEM(pre_act.shape, bf16),
                pltpu.VMEM(down_weight.shape, bf16),
            ),
            in_specs=[anywhere] * 3,
            out_specs=(pl.BlockSpec(memory_space=pltpu.VMEM),) * 2,
            scratch_shapes=[
                pltpu.VMEM((total, rows, width), bf16),
                pltpu.VMEM((total, rows // 2, width), bf16),
                pltpu.VMEM((total, rows // 2, width), bf16),
                pltpu.VMEM((depths, tiles, rows, width), bf16),
                pltpu.VMEM((tiles, depths * rows, width), bf16),
                pltpu.VMEM((depths * rows, features), bf16),
                dma((tiles,)), dma((total,)), dma((depths,)),
                dma((total,)), dma((total,)), dma((total,)), dma((total,)), dma((total,)), dma,
                dma((depths,)), dma, dma, dma, dma, dma, dma, dma,
            ],
            compiler_params=pltpu.CompilerParams(
                collective_id=0, has_side_effects=True, vmem_limit_bytes=40 * 1024 * 1024
            ),
        )(grad_out, pre_act, down_weight)
        return write_out(results)

    return jax.shard_map(
        on_device,
        mesh=mesh,
        in_specs=(P("depth", "col"), P("depth", "row"), P(("row", "depth"), "col")),
        out_specs=(P("depth", "row"), P(("row", "depth"), "col")),
        check_vma=False,
    )
```

time: 166 us -> 160 us (0.964)
  Pallas kernels: 165 us -> 160 us
    pallas_call x1, Pallas kernels: 160 us -> 154 us  [on_device(): pl.pallas_call(functools.partial(kernel, depths, width), out_shape=(pltpu...]
where the time goes in v3:
time: 160 us
  Pallas kernels  160 us (100%)
    pallas_call x1, Pallas kernels, on_device(): pl.pallas_call(functools.partial(kernel, depths, width), out_shape=(pltpu...  154 us
    pallas_call x1, Pallas kernels, write_out(): pl.pallas_call(body, out_shape=tuple((jax.ShapeDtypeStruct(r.shape, r.dty...  5.65 us

profile of v3, /device:TPU:0, one launch (start us, length us, event | category | flops | bytes accessed | tf_op | source)
XLA Modules:
  0.0 160.2 jit_solution(14409742589577898285)
XLA Ops:
  0.6 153.9 %shard_map.50 = (bf16[256,12288]{1,0:T(8,128)(2,1)S(1)}, bf16[3072,1536]{1,0:T(8,128)(2,1)S(1)}) custom-call(bf16[256,1536]{1,0:T(8,128)(2,1)} %grad_ref.1, bf16[256,12288]{1,0:T(8,128)(2,1)} %pre_ref.1, bf16[3072,1536]{1,0:T(8,128)(2,1)} %weight_ref.1), custom_call_target="tpu_custom_call" | custom-call | tf_op jit(solution)/shard_map/pallas_call | solution.py:376
  154.6 5.7 %shard_map.51 = (bf16[256,12288]{1,0:T(8,128)(2,1)}, bf16[3072,1536]{1,0:T(8,128)(2,1)}) custom-call(bf16[256,12288]{1,0:T(8,128)(2,1)S(1)} %get-tuple-element.4.first, bf16[3072,1536]{1,0:T(8,128)(2,1)S(1)} %get-tuple-element.5.second), custom_call_target="tpu_custom_call" | custom-call | tf_op jit(solution)/shard_map/pallas_call | solution.py:353

commit v4 on v3

--- a/solution.py
+++ b/solution.py
@@ -11,7 +11,8 @@
 sqrt_two_pi = 0.7978845608028654
 cubic_coeff = 0.044715
 HOP = 3
-FINISH = 12
+FINISH = 18
+PIECES = 2
 
 
 def gelu_value(preact):
@@ -184,7 +185,7 @@
 
         by_rows(half, body)
 
-    turns = max(2 * total + 1 + HOP, total + FINISH + 2 * tiles)
+    turns = max(2 * total + 1 + HOP, total + FINISH + PIECES * tiles)
 
     @pl.loop(0, turns)
     def _(i):
@@ -302,11 +303,13 @@
 
         late = i - total - FINISH
 
-        @pl.when((late >= 0) & (lax.rem(late, 2) == 0) & (late < 2 * tiles))
-        def _():
-            tile = lax.div(late, 2)
-            weight[tile_rows(tile), :] = lax.dot_general(
-                act[tile], grad[...], (((0,), (0,)), ((), ())),
+        @pl.when((late >= 0) & (late < PIECES * tiles))
+        def _():
+            tile = lax.div(late, jnp.int32(PIECES))
+            size = weight.shape[1] // PIECES
+            which = lines(lax.rem(late, jnp.int32(PIECES)) * size, size)
+            weight[tile_rows(tile), which] = lax.dot_general(
+                act[tile], grad[:, which], (((0,), (0,)), ((), ())),
                 preferred_element_type=jnp.float32,
             ).astype(jnp.bfloat16)
 
@@ -335,7 +338,7 @@
 
 
 def write_out(results):
-    parts = 4
+    parts = 16
 
     def body(first, second, first_out, second_out, sems):
         copies = []

time: 160 us -> 158 us (0.988)
  Pallas kernels: 160 us -> 157 us
    pallas_call x1, Pallas kernels: 154 us -> 152 us  [on_device(): pl.pallas_call(functools.partial(kernel, depths, width), out_shape=(pltpu...]
where the time goes in v4:
time: 158 us
  Pallas kernels  157 us (99%)
    pallas_call x1, Pallas kernels, on_device(): pl.pallas_call(functools.partial(kernel, depths, width), out_shape=(pltpu...  152 us
    pallas_call x1, Pallas kernels, write_out(): pl.pallas_call(body, out_shape=tuple((jax.ShapeDtypeStruct(r.shape, r.dty...  5.77 us

profile of v4, /device:TPU:0, one launch (start us, length us, event | category | flops | bytes accessed | tf_op | source)
XLA Modules:
  0.0 158.0 jit_solution(6726205315573638124)
XLA Ops:
  0.6 151.6 %shard_map.50 = (bf16[256,12288]{1,0:T(8,128)(2,1)S(1)}, bf16[3072,1536]{1,0:T(8,128)(2,1)S(1)}) custom-call(bf16[256,1536]{1,0:T(8,128)(2,1)} %grad_ref.1, bf16[256,12288]{1,0:T(8,128)(2,1)} %pre_ref.1, bf16[3072,1536]{1,0:T(8,128)(2,1)} %weight_ref.1), custom_call_target="tpu_custom_call" | custom-call | tf_op jit(solution)/shard_map/pallas_call | solution.py:379
  152.3 5.8 %shard_map.51 = (bf16[256,12288]{1,0:T(8,128)(2,1)}, bf16[3072,1536]{1,0:T(8,128)(2,1)}) custom-call(bf16[256,12288]{1,0:T(8,128)(2,1)S(1)} %get-tuple-element.4.first, bf16[3072,1536]{1,0:T(8,128)(2,1)S(1)} %get-tuple-element.5.second), custom_call_target="tpu_custom_call" | custom-call | tf_op jit(solution)/shard_map/pallas_call | solution.py:356

commit v5 on v4

--- a/solution.py
+++ b/solution.py
@@ -166,7 +166,7 @@
         send_grad(s).start()
     load_grad(0).wait()
 
-    step = 32
+    step = 64
 
     def by_rows(count, body):
         @pl.loop(0, count // step)
@@ -185,13 +185,14 @@
 
         by_rows(half, body)
 
-    turns = max(2 * total + 1 + HOP, total + FINISH + PIECES * tiles)
+    finish_lag = min(FINISH, total - 1)
+    turns = max(2 * total + 1 + HOP, total + finish_lag + PIECES * tiles)
 
     @pl.loop(0, turns)
     def _(i):
         inward = i - 1
         outward = inward - HOP
-        ended = i - FINISH
+        ended = i - finish_lag
         given = i - total
         spread = given - 1
         passed = spread - HOP
@@ -301,7 +302,7 @@
 
             by_rows(rows, body)
 
-        late = i - total - FINISH
+        late = i - total - finish_lag
 
         @pl.when((late >= 0) & (late < PIECES * tiles))
         def _():

time: 158 us -> 158 us (level)
  no operation moved by 1% of the time
where the time goes in v5:
time: 158 us
  Pallas kernels  157 us (99%)
    pallas_call x1, Pallas kernels, on_device(): pl.pallas_call(functools.partial(kernel, depths, width), out_shape=(pltpu...  152 us
    pallas_call x1, Pallas kernels, write_out(): pl.pallas_call(body, out_shape=tuple((jax.ShapeDtypeStruct(r.shape, r.dty...  5.77 us

profile of v5, /device:TPU:0, one launch (start us, length us, event | category | flops | bytes accessed | tf_op | source)
XLA Modules:
  0.0 158.0 jit_solution(10395968762482104261)
XLA Ops:
  0.6 151.6 %shard_map.50 = (bf16[256,12288]{1,0:T(8,128)(2,1)S(1)}, bf16[3072,1536]{1,0:T(8,128)(2,1)S(1)}) custom-call(bf16[256,1536]{1,0:T(8,128)(2,1)} %grad_ref.1, bf16[256,12288]{1,0:T(8,128)(2,1)} %pre_ref.1, bf16[3072,1536]{1,0:T(8,128)(2,1)} %weight_ref.1), custom_call_target="tpu_custom_call" | custom-call | tf_op jit(solution)/shard_map/pallas_call | solution.py:380
  152.2 5.8 %shard_map.51 = (bf16[256,12288]{1,0:T(8,128)(2,1)}, bf16[3072,1536]{1,0:T(8,128)(2,1)}) custom-call(bf16[256,12288]{1,0:T(8,128)(2,1)S(1)} %get-tuple-element.4.first, bf16[3072,1536]{1,0:T(8,128)(2,1)S(1)} %get-tuple-element.5.second), custom_call_target="tpu_custom_call" | custom-call | tf_op jit(solution)/shard_map/pallas_call | solution.py:357

commit v6 on v4

--- a/solution.py
+++ b/solution.py
@@ -347,8 +347,8 @@
                 size = src.shape[0] // parts
                 piece = pl.ds(k * size, size)
                 copies.append(pltpu.make_async_copy(src.at[piece], dst.at[piece], sems.at[n, k]))
-        for copy in copies:
-            copy.start()
+        for k, copy in enumerate(copies):
+            copy.start(priority=k % 2)
         for copy in copies:
             copy.wait()
 

time: 158 us -> 158 us (level)
  no operation moved by 1% of the time
where the time goes in v6:
time: 158 us
  Pallas kernels  157 us (99%)
    pallas_call x1, Pallas kernels, on_device(): pl.pallas_call(functools.partial(kernel, depths, width), out_shape=(pltpu...  152 us
    pallas_call x1, Pallas kernels, write_out(): pl.pallas_call(body, out_shape=tuple((jax.ShapeDtypeStruct(r.shape, r.dty...  5.77 us

profile of v6, /device:TPU:0, one launch (start us, length us, event | category | flops | bytes accessed | tf_op | source)
XLA Modules:
  0.0 158.0 jit_solution(7194031719011607039)
XLA Ops:
  0.6 151.6 %shard_map.50 = (bf16[256,12288]{1,0:T(8,128)(2,1)S(1)}, bf16[3072,1536]{1,0:T(8,128)(2,1)S(1)}) custom-call(bf16[256,1536]{1,0:T(8,128)(2,1)} %grad_ref.1, bf16[256,12288]{1,0:T(8,128)(2,1)} %pre_ref.1, bf16[3072,1536]{1,0:T(8,128)(2,1)} %weight_ref.1), custom_call_target="tpu_custom_call" | custom-call | tf_op jit(solution)/shard_map/pallas_call | solution.py:379
  152.3 5.8 %shard_map.51 = (bf16[256,12288]{1,0:T(8,128)(2,1)}, bf16[3072,1536]{1,0:T(8,128)(2,1)}) custom-call(bf16[256,12288]{1,0:T(8,128)(2,1)S(1)} %get-tuple-element.4.first, bf16[3072,1536]{1,0:T(8,128)(2,1)S(1)} %get-tuple-element.5.second), custom_call_target="tpu_custom_call" | custom-call | tf_op jit(solution)/shard_map/pallas_call | solution.py:356
